TPU v7x, 32 devices: a whole 2x2x4 slice. The times are simulated.
32 devices in a mesh: groups: 2 (over y), seq: 4 (over z), head: 4 (over x, core).
Axes of the slice: x: 2, y: 2, z: 4, core: 2. Of those that a mesh axis runs over, the one named last changes fastest.
Arguments:
- queries: bfloat16 [2048, 8192], P(('groups', 'seq'), 'head'), parts along dimension 0, may hold values from -16 to 16
- keys: bfloat16 [2048, 1024], P(('groups', 'seq'), 'head'), parts along dimension 0, may hold values from -16 to 16
- values: bfloat16 [2048, 1024], P(('groups', 'seq'), 'head'), parts along dimension 0, may hold values from -6 to 6
- prompt_len: int32 [2], P('groups'), parts along dimension 0, may hold values from 256 to 1024
- page_dest: int32 [8, 2], P('groups'), parts along dimension 0, may hold values from 0 to 3, all different within a row; in each aligned block of 4 rows (0 to 3, 4 to 7, ...) at most 4 rows name the same one
Outputs:
- attended: bfloat16 [2048, 8192], P(('groups', 'seq'), 'head'), parts along dimension 0
- decode_page_cache: bfloat16 [32, 128, 2048], P(('groups', 'seq'), None, 'head'), parts along dimension 0
There are 2 independent parts, one for each index of `groups`. A program takes and returns all parts, laid end to end along the dimension named above; each array names one. Nothing has to cross between parts.
Inputs may be any that keep to these rules, and one draw needn't show every extreme that they name: `page_dest`: row s names the decode devices of the 2 pages of tokens s * 256 to (s + 1) * 256 - 1, all different within a row; no device is named more than 4 times in all, and some device exactly 4 times.
All inputs are finite; a program needn't handle non-finite values.
Results may differ from a plain program's by a relative error of at most 0.005.
Values may be sent and summed in bfloat16 or wider, within the bound.
A program may use at most 64 MiB of HBM per device.

v0:
```python
import functools
import math

import jax
import jax.numpy as jnp
from jax import lax
from jax.experimental import pallas as pl
from jax.experimental.pallas import tpu as pltpu
from jax.sharding import PartitionSpec as P

HEAD = 128
PAGE = 128
NEG = -1e30
MESH = pl.DeviceIdType.MESH


def kernel(
    n, kv_heads, group, slots,
    plen_ref, dest_ref, q_hbm, k_hbm, v_hbm,
    att_ref, cache_ref,
    q_ref, kv, m_ref, acc_ref, p_ref, slot_ref,
    q_sem, own_sem, up_send, down_send, recv_sem,
):
    me = lax.axis_index("seq")
    rows = q_ref.shape[0]
    chunks = 2 * kv_heads
    ppd = rows // PAGE
    coef = math.log2(math.e) / math.sqrt(HEAD)

    def own_copy(c):
        src = k_hbm if c % 2 == 0 else v_hbm
        return pltpu.make_async_copy(
            src.at[:, pl.ds((c // 2) * HEAD, HEAD)], kv.at[me, c], own_sem.at[c]
        )

    q_copy = pltpu.make_async_copy(q_hbm, q_ref, q_sem)
    for c in range(chunks):
        own_copy(c).start()
    q_copy.start()

    barrier = pltpu.get_barrier_semaphore()

    @pl.when(me > 0)
    def _():
        pl.semaphore_signal(barrier, inc=1, device_id={"seq": me - 1}, device_id_type=MESH)

    @pl.when(me < n - 1)
    def _():
        pl.semaphore_signal(barrier, inc=1, device_id={"seq": me + 1}, device_id_type=MESH)

    pl.semaphore_wait(barrier, jnp.minimum(me, 1) + jnp.minimum(n - 1 - me, 1))

    def up(blk, c):
        return pltpu.make_async_remote_copy(
            src_ref=kv.at[blk, c], dst_ref=kv.at[blk, c],
            send_sem=up_send.at[blk, c], recv_sem=recv_sem.at[blk, c],
            device_id={"seq": me + 1}, device_id_type=MESH,
        )

    def down(blk, c):
        return pltpu.make_async_remote_copy(
            src_ref=kv.at[blk, c], dst_ref=kv.at[blk, c],
            send_sem=down_send.at[blk, c], recv_sem=recv_sem.at[blk, c],
            device_id={"seq": me - 1}, device_id_type=MESH,
        )

    for c in range(chunks):
        own_copy(c).wait()

        @pl.when(me < n - 1)
        def _():
            up(me, c).start()

        @pl.when(me > 0)
        def _():
            down(me, c).start()

    end = plen_ref[0]

    def rank(page, seen):
        hit = dest_ref[page // ppd, page % ppd] == me
        slot_ref[page] = jnp.where(hit, seen, -1)
        return seen + jnp.where(hit, 1, 0)

    lax.fori_loop(0, n * ppd, rank, jnp.int32(0))
    cache_ref[...] = jnp.zeros_like(cache_ref)
    token = lax.broadcasted_iota(jnp.int32, (PAGE, HEAD), 0)

    def store_pages(blk, c):
        lane = pl.ds(c * HEAD, HEAD)
        for k in range(ppd):
            number = blk * ppd + k
            page = kv[blk, c, k * PAGE:(k + 1) * PAGE, :]
            for r in range(slots):
                limit = jnp.where(slot_ref[number] == r, end - number * PAGE, 0)
                cache_ref[r, :, lane] = jnp.where(token < limit, page, cache_ref[r, :, lane])

    q_copy.wait()

    def cols(h):
        return pl.ds(pl.multiple_of(h * HEAD, HEAD), HEAD)

    def scores(g, h, blk):
        q = q_ref[:, cols(h)]
        return lax.dot_general(
            q, kv[blk, 2 * g], (((1,), (1,)), ((), ())), preferred_element_type=jnp.float32
        )

    def weigh(p, g, blk):
        v = kv[blk, 2 * g + 1]
        v = jnp.concatenate([v, jnp.ones_like(v)], axis=1)
        return jnp.dot(p, v, preferred_element_type=jnp.float32)

    causal = lax.broadcasted_iota(jnp.int32, (rows, rows), 1) <= lax.broadcasted_iota(
        jnp.int32, (rows, rows), 0
    )

    def diagonal(g):
        @pl.loop(0, group, unroll=2)
        def _(i):
            h = g * group + i
            s = jnp.where(causal, scores(g, h, me), NEG)
            m = jnp.max(s, axis=1, keepdims=True)
            p = jnp.exp2((s - m) * coef)
            m_ref[h] = jnp.broadcast_to(m, (rows, HEAD))
            acc_ref[h] = weigh(p.astype(jnp.bfloat16), g, me)

    for g in range(kv_heads):
        diagonal(g)
    for c in range(chunks):
        store_pages(me, c)

    def pass_k(g, blk):
        @pl.loop(0, group, unroll=2)
        def _(i):
            h = g * group + i
            s = scores(g, h, blk)
            old = m_ref[h]
            new = jnp.maximum(old, jnp.max(s, axis=1, keepdims=True))
            p = jnp.exp2((s - jnp.concatenate([new] * (rows // HEAD), axis=1)) * coef)
            factor = jnp.exp2((old - new) * coef)
            m_ref[h] = new
            p_ref[i] = p.astype(jnp.bfloat16)
            acc_ref[h] = acc_ref[h] * jnp.concatenate([factor, factor], axis=1)

    def pass_v(g, blk):
        @pl.loop(0, group, unroll=2)
        def _(i):
            h = g * group + i
            acc_ref[h] = acc_ref[h] + weigh(p_ref[i], g, blk)

    def step(t, c):
        @pl.when(me >= t)
        def _():
            up(me - t, c).wait_recv()

            @pl.when(me < n - 1)
            def _():
                up(me - t, c).start()

        @pl.when(me + t < n)
        def _():
            down(me + t, c).wait_recv()

            @pl.when(me > 0)
            def _():
                down(me + t, c).start()

            store_pages(me + t, c)

        @pl.when(me >= t)
        def _():
            store_pages(me - t, c)
            if c % 2 == 0:
                pass_k(c // 2, me - t)
            else:
                pass_v(c // 2, me - t)

    @pl.loop(1, n)
    def _(t):
        for c in range(chunks):
            step(t, c)

    live = (
        me * rows + lax.broadcasted_iota(jnp.int32, (rows, HEAD), 0)
    ) < end

    @pl.loop(0, kv_heads * group, unroll=2)
    def _(h):
        out = jnp.where(live, acc_ref[h, :, :HEAD] / acc_ref[h, :, HEAD:], 0.0)
        att_ref[:, cols(h)] = out.astype(jnp.bfloat16)

    @pl.loop(0, n)
    def _(blk):
        @pl.loop(0, chunks)
        def _(c):
            @pl.when((blk <= me) & (me < n - 1))
            def _():
                up(blk, c).wait_send()

            @pl.when((blk >= me) & (me > 0))
            def _():
                down(blk, c).wait_send()


def local(n, queries, keys, values, prompt_len, page_dest):
    rows, width = queries.shape
    kv_heads = keys.shape[1] // HEAD
    heads = width // HEAD
    group = heads // kv_heads
    slots = 2 * page_dest.shape[1]
    chunks = 2 * kv_heads
    hbm = pl.BlockSpec(memory_space=pltpu.HBM)
    vmem = pl.BlockSpec(memory_space=pltpu.VMEM)
    smem = pl.BlockSpec(memory_space=pltpu.SMEM)
    return pl.pallas_call(
        functools.partial(kernel, n, kv_heads, group, slots),
        out_shape=(
            jax.ShapeDtypeStruct((rows, width), jnp.bfloat16),
            jax.ShapeDtypeStruct((slots, PAGE, chunks * HEAD), jnp.bfloat16),
        ),
        in_specs=[smem, smem, hbm, hbm, hbm],
        out_specs=(vmem, vmem),
        scratch_shapes=[
            pltpu.VMEM((rows, width), jnp.bfloat16),
            pltpu.VMEM((n, chunks, rows, HEAD), jnp.bfloat16),
            pltpu.VMEM((heads, rows, HEAD), jnp.float32),
            pltpu.VMEM((heads, rows, 2 * HEAD), jnp.float32),
            pltpu.VMEM((group, rows, rows), jnp.bfloat16),
            pltpu.SMEM((n * rows // PAGE,), jnp.int32),
            pltpu.SemaphoreType.DMA,
            pltpu.SemaphoreType.DMA((chunks,)),
            pltpu.SemaphoreType.DMA((n, chunks)),
            pltpu.SemaphoreType.DMA((n, chunks)),
            pltpu.SemaphoreType.DMA((n, chunks)),
        ],
        compiler_params=pltpu.CompilerParams(
            collective_id=0, has_side_effects=True, vmem_limit_bytes=48 * 1024 * 1024
        ),
    )(prompt_len, page_dest, queries, keys, values)


def solution(mesh):
    return jax.shard_map(
        functools.partial(local, mesh.shape["seq"]),
        mesh=mesh,
        in_specs=(
            P(("groups", "seq"), "head"),
            P(("groups", "seq"), "head"),
            P(("groups", "seq"), "head"),
            P("groups"),
            P("groups", None),
        ),
        out_specs=(P(("groups", "seq"), "head"), P(("groups", "seq"), None, "head")),
        check_vma=False,
    )
```

profile of v0, /device:TPU:0, one launch (start us, length us, event | category | flops | bytes accessed | tf_op | source)
XLA Modules:
  0.0 29.9 jit_solution(17766420560694985902)
XLA Ops:
  0.6 0.0 copy-start.3
  1.3 0.0 copy-done.3
  1.3 0.1 copy.7.dest_ref
  1.4 0.0 copy-start
  1.4 1.2 %copy-done = bf16[256,2048]{1,0:T(8,128)(2,1)S(1)} copy-done((bf16[256,2048]{1,0:T(8,128)(2,1)S(1)}, bf16[256,2048]{1,0:T(8,128)(2,1)}, u32[]{:S(2)}) %copy-start) | copy-done | bytes 1048600
  2.6 0.0 copy-start.1
  2.6 0.9 %copy-done.1 = bf16[256,256]{1,0:T(8,128)(2,1)S(1)} copy-done((bf16[256,256]{1,0:T(8,128)(2,1)S(1)}, bf16[256,256]{1,0:T(8,128)(2,1)}, u32[]{:S(2)}) %copy-start.1) | copy-done | bytes 131096
  3.5 0.0 copy-start.2
  3.5 0.9 %copy-done.2 = bf16[256,256]{1,0:T(8,128)(2,1)S(1)} copy-done((bf16[256,256]{1,0:T(8,128)(2,1)S(1)}, bf16[256,256]{1,0:T(8,128)(2,1)}, u32[]{:S(2)}) %copy-start.2) | copy-done | bytes 131096
  4.4 23.7 %shard_map.68 = (bf16[256,2048]{1,0:T(8,128)(2,1)S(1)}, bf16[4,128,512]{2,1,0:T(8,128)(2,1)S(1)}) custom-call(s32[1]{0:T(128)S(6)} %copy.10.plen_ref, s32[4,2]{1,0:T(4,128)S(1)} %copy.7.dest_ref, bf16[256,2048]{1,0:T(8,128)(2,1)S(1)} %copy-done, bf16[256,256]{1,0:T(8,128)(2,1)S(1)} %copy-done.1, bf16[256,256]{1,0:T(8,128)(2,1)S(1)} %copy-done.2), custom_call_target="tpu_custom_call" | custom-call | tf_op jit(solution)/shard_map/pallas_call | solution.py:216
  28.1 1.0 %copy.11 = bf16[256,2048]{1,0:T(8,128)(2,1)} copy(bf16[256,2048]{1,0:T(8,128)(2,1)S(1)} %get-tuple-element.4) | data formatting | bytes 2097152
  29.1 0.8 %copy.12 = bf16[4,128,512]{2,1,0:T(8,128)(2,1)} copy(bf16[4,128,512]{2,1,0:T(8,128)(2,1)S(1)} %get-tuple-element.5) | data formatting | bytes 1048576
Async XLA Ops:
  0.6 0.7 %copy-start.3 = (s32[4,2]{0,1:T(2,128)S(1)}, s32[4,2]{0,1:T(2,128)}, u32[]{:S(2)}) copy-start(s32[4,2]{0,1:T(2,128)} %param.9) | copy-start | bytes 100
  1.4 1.2 %copy-start = (bf16[256,2048]{1,0:T(8,128)(2,1)S(1)}, bf16[256,2048]{1,0:T(8,128)(2,1)}, u32[]{:S(2)}) copy-start(bf16[256,2048]{1,0:T(8,128)(2,1)} %q_hbm.1) | copy-start | bytes 3145732
  2.6 0.9 %copy-start.1 = (bf16[256,256]{1,0:T(8,128)(2,1)S(1)}, bf16[256,256]{1,0:T(8,128)(2,1)}, u32[]{:S(2)}) copy-start(bf16[256,256]{1,0:T(8,128)(2,1)} %k_hbm.1) | copy-start | bytes 393220
  3.5 0.9 %copy-start.2 = (bf16[256,256]{1,0:T(8,128)(2,1)S(1)}, bf16[256,256]{1,0:T(8,128)(2,1)}, u32[]{:S(2)}) copy-start(bf16[256,256]{1,0:T(8,128)(2,1)} %v_hbm.1) | copy-start | bytes 393220
where the time goes:
time: 30.1 us; the launch traced here: 29.9 us
  Pallas kernels  23.7 us (79%)
  local copies, waits for them, and re-layouts  4.9 us (16%)
  between operations  1.31 us (4%)
    pallas_call x1, Pallas kernels, local(): pl.pallas_call(functools.partial(kernel, n, kv_heads, group, slots), out_...  23.7 us
    unnamed x11, local copies, waits for them, and re-layouts  4.9 us

commit v1 on v0

--- a/solution.py
+++ b/solution.py
@@ -16,10 +16,10 @@
 
 def kernel(
     n, kv_heads, group, slots,
-    plen_ref, dest_ref, q_hbm, k_hbm, v_hbm,
+    plen_ref, dest_hbm, q_hbm, k_hbm, v_hbm,
     att_ref, cache_ref,
-    q_ref, kv, m_ref, acc_ref, p_ref, slot_ref,
-    q_sem, own_sem, up_send, down_send, recv_sem,
+    q_ref, kv, m_ref, acc_ref, p_ref, slot_ref, dest_ref,
+    q_sem, own_sem, up_send, down_send, recv_sem, dest_sem,
 ):
     me = lax.axis_index("seq")
     rows = q_ref.shape[0]
@@ -37,6 +37,8 @@
     for c in range(chunks):
         own_copy(c).start()
     q_copy.start()
+    dest_copy = pltpu.make_async_copy(dest_hbm, dest_ref, dest_sem)
+    dest_copy.start()
 
     barrier = pltpu.get_barrier_semaphore()
 
@@ -75,10 +77,12 @@
         def _():
             down(me, c).start()
 
+    dest_copy.wait()
     end = plen_ref[0]
+    live = (me * rows + lax.broadcasted_iota(jnp.int32, (rows, HEAD), 0)) < end
 
     def rank(page, seen):
-        hit = dest_ref[page // ppd, page % ppd] == me
+        hit = dest_ref[page % ppd, page // ppd] == me
         slot_ref[page] = jnp.where(hit, seen, -1)
         return seen + jnp.where(hit, 1, 0)
 
@@ -114,6 +118,10 @@
     causal = lax.broadcasted_iota(jnp.int32, (rows, rows), 1) <= lax.broadcasted_iota(
         jnp.int32, (rows, rows), 0
     )
+
+    def finish(h, total):
+        out = jnp.where(live, total[:, :HEAD] / total[:, HEAD:], 0.0)
+        att_ref[:, cols(h)] = out.astype(jnp.bfloat16)
 
     def diagonal(g):
         @pl.loop(0, group, unroll=2)
@@ -127,6 +135,13 @@
 
     for g in range(kv_heads):
         diagonal(g)
+
+    @pl.when(me == 0)
+    def _():
+        @pl.loop(0, kv_heads * group)
+        def _(h):
+            finish(h, acc_ref[h])
+
     for c in range(chunks):
         store_pages(me, c)
 
@@ -143,11 +158,15 @@
             p_ref[i] = p.astype(jnp.bfloat16)
             acc_ref[h] = acc_ref[h] * jnp.concatenate([factor, factor], axis=1)
 
-    def pass_v(g, blk):
+    def pass_v(g, blk, last):
         @pl.loop(0, group, unroll=2)
         def _(i):
             h = g * group + i
-            acc_ref[h] = acc_ref[h] + weigh(p_ref[i], g, blk)
+            total = acc_ref[h] + weigh(p_ref[i], g, blk)
+            if last:
+                finish(h, total)
+            else:
+                acc_ref[h] = total
 
     def step(t, c):
         @pl.when(me >= t)
@@ -174,21 +193,19 @@
             if c % 2 == 0:
                 pass_k(c // 2, me - t)
             else:
-                pass_v(c // 2, me - t)
+
+                @pl.when(me > t)
+                def _():
+                    pass_v(c // 2, me - t, False)
+
+                @pl.when(me == t)
+                def _():
+                    pass_v(c // 2, me - t, True)
 
     @pl.loop(1, n)
     def _(t):
         for c in range(chunks):
             step(t, c)
-
-    live = (
-        me * rows + lax.broadcasted_iota(jnp.int32, (rows, HEAD), 0)
-    ) < end
-
-    @pl.loop(0, kv_heads * group, unroll=2)
-    def _(h):
-        out = jnp.where(live, acc_ref[h, :, :HEAD] / acc_ref[h, :, HEAD:], 0.0)
-        att_ref[:, cols(h)] = out.astype(jnp.bfloat16)
 
     @pl.loop(0, n)
     def _(blk):
@@ -201,6 +218,15 @@
             @pl.when((blk >= me) & (me > 0))
             def _():
                 down(blk, c).wait_send()
+
+
+def write_out(att_ref, cache_ref, att_hbm, cache_hbm, sem):
+    att_copy = pltpu.make_async_copy(att_ref, att_hbm, sem.at[0])
+    cache_copy = pltpu.make_async_copy(cache_ref, cache_hbm, sem.at[1])
+    att_copy.start()
+    cache_copy.start()
+    att_copy.wait()
+    cache_copy.wait()
 
 
 def local(n, queries, keys, values, prompt_len, page_dest):
@@ -211,15 +237,15 @@
     slots = 2 * page_dest.shape[1]
     chunks = 2 * kv_heads
     hbm = pl.BlockSpec(memory_space=pltpu.HBM)
+    smem = pl.BlockSpec(memory_space=pltpu.SMEM)
     vmem = pl.BlockSpec(memory_space=pltpu.VMEM)
-    smem = pl.BlockSpec(memory_space=pltpu.SMEM)
-    return pl.pallas_call(
+    att, cache = pl.pallas_call(
         functools.partial(kernel, n, kv_heads, group, slots),
         out_shape=(
             jax.ShapeDtypeStruct((rows, width), jnp.bfloat16),
             jax.ShapeDtypeStruct((slots, PAGE, chunks * HEAD), jnp.bfloat16),
         ),
-        in_specs=[smem, smem, hbm, hbm, hbm],
+        in_specs=[smem] + [hbm] * 4,
         out_specs=(vmem, vmem),
         scratch_shapes=[
             pltpu.VMEM((rows, width), jnp.bfloat16),
@@ -228,16 +254,32 @@
             pltpu.VMEM((heads, rows, 2 * HEAD), jnp.float32),
             pltpu.VMEM((group, rows, rows), jnp.bfloat16),
             pltpu.SMEM((n * rows // PAGE,), jnp.int32),
+            pltpu.SMEM(page_dest.shape[::-1], jnp.int32),
             pltpu.SemaphoreType.DMA,
             pltpu.SemaphoreType.DMA((chunks,)),
             pltpu.SemaphoreType.DMA((n, chunks)),
             pltpu.SemaphoreType.DMA((n, chunks)),
             pltpu.SemaphoreType.DMA((n, chunks)),
+            pltpu.SemaphoreType.DMA,
         ],
         compiler_params=pltpu.CompilerParams(
             collective_id=0, has_side_effects=True, vmem_limit_bytes=48 * 1024 * 1024
         ),
-    )(prompt_len, page_dest, queries, keys, values)
+    )(prompt_len, *(
+        pltpu.with_memory_space_constraint(x, pltpu.HBM)
+        for x in (page_dest.T, queries, keys, values)
+    ))
+    return pl.pallas_call(
+        write_out,
+        out_shape=(
+            jax.ShapeDtypeStruct(att.shape, att.dtype),
+            jax.ShapeDtypeStruct(cache.shape, cache.dtype),
+        ),
+        in_specs=[vmem, vmem],
+        out_specs=(hbm, hbm),
+        scratch_shapes=[pltpu.SemaphoreType.DMA((2,))],
+        compiler_params=pltpu.CompilerParams(vmem_limit_bytes=8 * 1024 * 1024),
+    )(att, cache)
 
 
 def solution(mesh):

time: 30.1 us -> 25.2 us (0.84)
  local copies, waits for them, and re-layouts: 4.9 us -> 0 us
    unnamed x11 -> x0, local copies, waits for them, and re-layouts: 4.9 us -> none
    pallas_call x0 -> x1, Pallas kernels: none -> 1.16 us  [local(): pl.pallas_call(write_out, out_shape=(jax.ShapeDtypeStruct(att.shape, att....]
    pallas_call x1, Pallas kernels: 23.7 us -> 22.6 us  [local(): pl.pallas_call(functools.partial(kernel, n, kv_heads, group, slots), out_...]
where the time goes in v1:
time: 25.2 us; the launch traced here: 25.1 us
  Pallas kernels  23.8 us (94%)
  between operations  1.29 us (5%)
    pallas_call x1, Pallas kernels, local(): pl.pallas_call(functools.partial(kernel, n, kv_heads, group, slots), out_...  22.6 us
    pallas_call x1, Pallas kernels, local(): pl.pallas_call(write_out, out_shape=(jax.ShapeDtypeStruct(att.shape, att....  1.16 us

profile of v1, /device:TPU:0, one launch (start us, length us, event | category | flops | bytes accessed | tf_op | source)
XLA Modules:
  0.0 25.1 jit_solution(15411086694681463195)
XLA Ops:
  1.3 22.6 %shard_map.68 = (bf16[256,2048]{1,0:T(8,128)(2,1)S(1)}, bf16[4,128,512]{2,1,0:T(8,128)(2,1)S(1)}) custom-call(s32[1]{0:T(128)S(6)} %copy.7.plen_ref, s32[2,4]{1,0:T(2,128)} %bitcast.1, bf16[256,2048]{1,0:T(8,128)(2,1)} %q_hbm.1, bf16[256,256]{1,0:T(8,128)(2,1)} %k_hbm.1, bf16[256,256]{1,0:T(8,128)(2,1)} %v_hbm.1), custom_call_target="tpu_custom_call" | custom-call | tf_op jit(solution)/shard_map/pallas_call | solution.py:242
  23.9 1.2 %shard_map.69 = (bf16[256,2048]{1,0:T(8,128)(2,1)}, bf16[4,128,512]{2,1,0:T(8,128)(2,1)}) custom-call(bf16[256,2048]{1,0:T(8,128)(2,1)S(1)} %get-tuple-element.4.att_ref, bf16[4,128,512]{2,1,0:T(8,128)(2,1)S(1)} %get-tuple-element.5.cache_ref), custom_call_target="tpu_custom_call" | custom-call | tf_op jit(solution)/shard_map/pallas_call | solution.py:272

commit v2 on v1

--- a/solution.py
+++ b/solution.py
@@ -18,7 +18,7 @@
     n, kv_heads, group, slots,
     plen_ref, dest_hbm, q_hbm, k_hbm, v_hbm,
     att_ref, cache_ref,
-    q_ref, kv, m_ref, acc_ref, p_ref, slot_ref, dest_ref,
+    q_ref, kv, m_ref, l_ref, acc_ref, p_ref, slot_ref, dest_ref,
     q_sem, own_sem, up_send, down_send, recv_sem, dest_sem,
 ):
     me = lax.axis_index("seq")
@@ -36,7 +36,6 @@
     q_copy = pltpu.make_async_copy(q_hbm, q_ref, q_sem)
     for c in range(chunks):
         own_copy(c).start()
-    q_copy.start()
     dest_copy = pltpu.make_async_copy(dest_hbm, dest_ref, dest_sem)
     dest_copy.start()
 
@@ -77,6 +76,7 @@
         def _():
             down(me, c).start()
 
+    q_copy.start()
     dest_copy.wait()
     end = plen_ref[0]
     live = (me * rows + lax.broadcasted_iota(jnp.int32, (rows, HEAD), 0)) < end
@@ -111,17 +111,20 @@
         )
 
     def weigh(p, g, blk):
-        v = kv[blk, 2 * g + 1]
-        v = jnp.concatenate([v, jnp.ones_like(v)], axis=1)
-        return jnp.dot(p, v, preferred_element_type=jnp.float32)
+        return jnp.dot(p, kv[blk, 2 * g + 1], preferred_element_type=jnp.float32)
+
+    def total(p):
+        return jnp.dot(p, jnp.ones((rows, HEAD), jnp.bfloat16), preferred_element_type=jnp.float32)
 
     causal = lax.broadcasted_iota(jnp.int32, (rows, rows), 1) <= lax.broadcasted_iota(
         jnp.int32, (rows, rows), 0
     )
 
-    def finish(h, total):
-        out = jnp.where(live, total[:, :HEAD] / total[:, HEAD:], 0.0)
-        att_ref[:, cols(h)] = out.astype(jnp.bfloat16)
+    def invert(h):
+        l_ref[h] = jnp.where(live, 1.0 / l_ref[h], 0.0)
+
+    def finish(h, value):
+        att_ref[:, cols(h)] = (value * l_ref[h]).astype(jnp.bfloat16)
 
     def diagonal(g):
         @pl.loop(0, group, unroll=2)
@@ -129,9 +132,10 @@
             h = g * group + i
             s = jnp.where(causal, scores(g, h, me), NEG)
             m = jnp.max(s, axis=1, keepdims=True)
-            p = jnp.exp2((s - m) * coef)
+            p = jnp.exp2((s - m) * coef).astype(jnp.bfloat16)
             m_ref[h] = jnp.broadcast_to(m, (rows, HEAD))
-            acc_ref[h] = weigh(p.astype(jnp.bfloat16), g, me)
+            l_ref[h] = total(p)
+            acc_ref[h] = weigh(p, g, me)
 
     for g in range(kv_heads):
         diagonal(g)
@@ -140,6 +144,7 @@
     def _():
         @pl.loop(0, kv_heads * group)
         def _(h):
+            invert(h)
             finish(h, acc_ref[h])
 
     for c in range(chunks):
@@ -153,20 +158,22 @@
             old = m_ref[h]
             new = jnp.maximum(old, jnp.max(s, axis=1, keepdims=True))
             p = jnp.exp2((s - jnp.concatenate([new] * (rows // HEAD), axis=1)) * coef)
+            p = p.astype(jnp.bfloat16)
             factor = jnp.exp2((old - new) * coef)
             m_ref[h] = new
-            p_ref[i] = p.astype(jnp.bfloat16)
-            acc_ref[h] = acc_ref[h] * jnp.concatenate([factor, factor], axis=1)
+            p_ref[i] = p
+            l_ref[h] = l_ref[h] * factor + total(p)
+            acc_ref[h] = acc_ref[h] * factor
 
     def pass_v(g, blk, last):
         @pl.loop(0, group, unroll=2)
         def _(i):
             h = g * group + i
-            total = acc_ref[h] + weigh(p_ref[i], g, blk)
+            value = acc_ref[h] + weigh(p_ref[i], g, blk)
             if last:
-                finish(h, total)
+                finish(h, value)
             else:
-                acc_ref[h] = total
+                acc_ref[h] = value
 
     def step(t, c):
         @pl.when(me >= t)
@@ -189,18 +196,24 @@
 
         @pl.when(me >= t)
         def _():
-            store_pages(me - t, c)
+            g = c // 2
             if c % 2 == 0:
-                pass_k(c // 2, me - t)
+                pass_k(g, me - t)
+
+                @pl.when(me == t)
+                def _():
+                    @pl.loop(0, group)
+                    def _(i):
+                        invert(g * group + i)
             else:
-
                 @pl.when(me > t)
                 def _():
-                    pass_v(c // 2, me - t, False)
+                    pass_v(g, me - t, False)
 
                 @pl.when(me == t)
                 def _():
-                    pass_v(c // 2, me - t, True)
+                    pass_v(g, me - t, True)
+            store_pages(me - t, c)
 
     @pl.loop(1, n)
     def _(t):
@@ -237,7 +250,6 @@
     slots = 2 * page_dest.shape[1]
     chunks = 2 * kv_heads
     hbm = pl.BlockSpec(memory_space=pltpu.HBM)
-    smem = pl.BlockSpec(memory_space=pltpu.SMEM)
     vmem = pl.BlockSpec(memory_space=pltpu.VMEM)
     att, cache = pl.pallas_call(
         functools.partial(kernel, n, kv_heads, group, slots),
@@ -245,13 +257,14 @@
             jax.ShapeDtypeStruct((rows, width), jnp.bfloat16),
             jax.ShapeDtypeStruct((slots, PAGE, chunks * HEAD), jnp.bfloat16),
         ),
-        in_specs=[smem] + [hbm] * 4,
+        in_specs=[pl.BlockSpec(memory_space=pltpu.SMEM)] + [hbm] * 4,
         out_specs=(vmem, vmem),
         scratch_shapes=[
             pltpu.VMEM((rows, width), jnp.bfloat16),
             pltpu.VMEM((n, chunks, rows, HEAD), jnp.bfloat16),
             pltpu.VMEM((heads, rows, HEAD), jnp.float32),
-            pltpu.VMEM((heads, rows, 2 * HEAD), jnp.float32),
+            pltpu.VMEM((heads, rows, HEAD), jnp.float32),
+            pltpu.VMEM((heads, rows, HEAD), jnp.float32),
             pltpu.VMEM((group, rows, rows), jnp.bfloat16),
             pltpu.SMEM((n * rows // PAGE,), jnp.int32),
             pltpu.SMEM(page_dest.shape[::-1], jnp.int32),

time: 25.2 us -> 33.8 us (1.34)
  the two profiles are of different devices: /device:TPU:0 before, /device:TPU:25 now
where the time goes in v2:
time: 33.8 us; the launch traced here: 33.7 us
  Pallas kernels  32.4 us (96%)
  between operations  1.29 us (4%)
    pallas_call x1, Pallas kernels, local(): pl.pallas_call(functools.partial(kernel, n, kv_heads, group, slots), out_...  31.2 us
    pallas_call x1, Pallas kernels, local(): pl.pallas_call(write_out, out_shape=(jax.ShapeDtypeStruct(att.shape, att....  1.16 us

profile of v2, /device:TPU:25, one launch (start us, length us, event | category | flops | bytes accessed | tf_op | source)
XLA Modules:
  0.0 33.7 jit_solution(11318251207355561059)
XLA Ops:
  1.3 31.2 %shard_map.68 = (bf16[256,2048]{1,0:T(8,128)(2,1)S(1)}, bf16[4,128,512]{2,1,0:T(8,128)(2,1)S(1)}) custom-call(s32[1]{0:T(128)S(6)} %copy.7.plen_ref, s32[2,4]{1,0:T(2,128)} %bitcast.1, bf16[256,2048]{1,0:T(8,128)(2,1)} %q_hbm.1, bf16[256,256]{1,0:T(8,128)(2,1)} %k_hbm.1, bf16[256,256]{1,0:T(8,128)(2,1)} %v_hbm.1), custom_call_target="tpu_custom_call" | custom-call | tf_op jit(solution)/shard_map/pallas_call | solution.py:254
  32.5 1.2 %shard_map.69 = (bf16[256,2048]{1,0:T(8,128)(2,1)}, bf16[4,128,512]{2,1,0:T(8,128)(2,1)}) custom-call(bf16[256,2048]{1,0:T(8,128)(2,1)S(1)} %get-tuple-element.4.att_ref, bf16[4,128,512]{2,1,0:T(8,128)(2,1)S(1)} %get-tuple-element.5.cache_ref), custom_call_target="tpu_custom_call" | custom-call | tf_op jit(solution)/shard_map/pallas_call | solution.py:285

commit v3 on v1

--- a/solution.py
+++ b/solution.py
@@ -36,7 +36,6 @@
     q_copy = pltpu.make_async_copy(q_hbm, q_ref, q_sem)
     for c in range(chunks):
         own_copy(c).start()
-    q_copy.start()
     dest_copy = pltpu.make_async_copy(dest_hbm, dest_ref, dest_sem)
     dest_copy.start()
 
@@ -77,6 +76,7 @@
         def _():
             down(me, c).start()
 
+    q_copy.start()
     dest_copy.wait()
     end = plen_ref[0]
     live = (me * rows + lax.broadcasted_iota(jnp.int32, (rows, HEAD), 0)) < end
@@ -159,7 +159,7 @@
             acc_ref[h] = acc_ref[h] * jnp.concatenate([factor, factor], axis=1)
 
     def pass_v(g, blk, last):
-        @pl.loop(0, group, unroll=2)
+        @pl.loop(0, group, unroll=4)
         def _(i):
             h = g * group + i
             total = acc_ref[h] + weigh(p_ref[i], g, blk)
@@ -189,8 +189,8 @@
 
         @pl.when(me >= t)
         def _():
-            store_pages(me - t, c)
             if c % 2 == 0:
+                store_pages(me - t, c)
                 pass_k(c // 2, me - t)
             else:
 
@@ -201,6 +201,7 @@
                 @pl.when(me == t)
                 def _():
                     pass_v(c // 2, me - t, True)
+                store_pages(me - t, c)
 
     @pl.loop(1, n)
     def _(t):

time: 25.2 us -> 25.5 us (1.012)
  Pallas kernels: 23.8 us -> 24.1 us
    pallas_call x1, Pallas kernels: 22.6 us -> 22.9 us  [local(): pl.pallas_call(functools.partial(kernel, n, kv_heads, group, slots), out_...]
where the time goes in v3:
time: 25.5 us; the launch traced here: 25.4 us
  Pallas kernels  24.1 us (95%)
  between operations  1.29 us (5%)
    pallas_call x1, Pallas kernels, local(): pl.pallas_call(functools.partial(kernel, n, kv_heads, group, slots), out_...  22.9 us
    pallas_call x1, Pallas kernels, local(): pl.pallas_call(write_out, out_shape=(jax.ShapeDtypeStruct(att.shape, att....  1.16 us

profile of v3, /device:TPU:0, one launch (start us, length us, event | category | flops | bytes accessed | tf_op | source)
XLA Modules:
  0.0 25.4 jit_solution(8010060013803506269)
XLA Ops:
  1.3 22.9 %shard_map.68 = (bf16[256,2048]{1,0:T(8,128)(2,1)S(1)}, bf16[4,128,512]{2,1,0:T(8,128)(2,1)S(1)}) custom-call(s32[1]{0:T(128)S(6)} %copy.7.plen_ref, s32[2,4]{1,0:T(2,128)} %bitcast.1, bf16[256,2048]{1,0:T(8,128)(2,1)} %q_hbm.1, bf16[256,256]{1,0:T(8,128)(2,1)} %k_hbm.1, bf16[256,256]{1,0:T(8,128)(2,1)} %v_hbm.1), custom_call_target="tpu_custom_call" | custom-call | tf_op jit(solution)/shard_map/pallas_call | solution.py:243
  24.2 1.2 %shard_map.69 = (bf16[256,2048]{1,0:T(8,128)(2,1)}, bf16[4,128,512]{2,1,0:T(8,128)(2,1)}) custom-call(bf16[256,2048]{1,0:T(8,128)(2,1)S(1)} %get-tuple-element.4.att_ref, bf16[4,128,512]{2,1,0:T(8,128)(2,1)S(1)} %get-tuple-element.5.cache_ref), custom_call_target="tpu_custom_call" | custom-call | tf_op jit(solution)/shard_map/pallas_call | solution.py:273
